TPU v7x, 32 devices: a whole 2x2x4 slice. The times are simulated.
32 devices in a mesh: layer: 8 (over y, x, core), dp: 4 (over z).
Axes of the slice: x: 2, y: 2, z: 4, core: 2. Of those that a mesh axis runs over, the one named last changes fastest.
Arguments:
- initial: float32 [256, 1024], P('dp'), may hold values from -6 to 6
- norm_gains: float32 [32, 1024], P('layer'), may hold values from 0.25 to 1.75
- first_weights: bfloat16 [32, 1024, 2048], P('layer'), may hold values from -0.1875 to 0.1875
- second_weights: bfloat16 [32, 2048, 1024], P('layer'), may hold values from -0.046875 to 0.046875
Outputs:
- layer_states: float32 [32, 256, 1024], P('layer', 'dp')
- residual_ratios: float32 [7], replicated
- coarse_defects_four: float32 [32, 256, 1024], P('layer', 'dp')
- coarse_defects_sixteen: float32 [32, 256, 1024], P('layer', 'dp')
All inputs are finite; a program needn't handle non-finite values.
Results may differ from a plain program's by a relative error of at most 0.02.
Values sent between devices are 32-bit elements; how exact they have to be, the bound alone decides.
A program may use at most 128 MiB of HBM per device.

v0:
```python
import jax
import jax.numpy as jnp
from jax import lax
from jax.sharding import PartitionSpec as P

epsilon = 1e-06


def shifted(block, axis, distance):
    devices = range(lax.axis_size(axis))
    route = [(i - distance, i) for i in devices if i - distance in devices]
    return lax.ppermute(block, axis, route)


def branch(row_block, weight_in, weight_out, gain_row):
    mean_square = jnp.mean(row_block * row_block, axis=-1, keepdims=True)
    normed = (row_block * lax.rsqrt(mean_square + epsilon) * gain_row).astype(jnp.bfloat16)
    hidden = jax.nn.gelu(
        jnp.dot(normed, weight_in, preferred_element_type=jnp.float32), approximate=True
    ).astype(jnp.bfloat16)
    return jnp.dot(hidden, weight_out, preferred_element_type=jnp.float32)


def local(initial, norm_gains, first_weights, second_weights):
    slot_count = first_weights.shape[0]
    sections = lax.axis_size("layer")
    layer_total = slot_count * sections
    norm_count = layer_total // 4 - 1
    first_point = lax.axis_index("layer") * slot_count
    points = first_point + jnp.arange(slot_count, dtype=jnp.int32) + 1
    spacings = (1, 4, 16)

    def shaped(flags, rank):
        return flags.reshape((slot_count,) + (1,) * (rank - 1))

    def previous(values, level_index):
        spacing = spacings[level_index]
        if spacing >= slot_count:
            portion = values
            distance = spacing // slot_count
        else:
            portion = values[slot_count - spacing :]
            distance = 1
        if level_index == 0:
            arrived = shifted(portion, "layer", distance)
        elif level_index == 1:
            arrived = shifted(portion, "layer", distance)
        else:
            arrived = shifted(portion, "layer", distance)
        if spacing < slot_count:
            arrived = jnp.concatenate([arrived, values[: slot_count - spacing]], axis=0)
        return arrived

    def incoming(values, level_index, anchor):
        arrived = previous(values, level_index)
        from_anchor = shaped(points - spacings[level_index] == 0, values.ndim)
        return jnp.where(from_anchor, anchor, arrived)

    def advance(before, level_index, active, right_side):
        factor = float(spacings[level_index])
        results = []
        for slot in range(slot_count):

            def advance_compute(values, source, slot=slot):
                return (
                    values
                    + factor
                    * branch(values, first_weights[slot], second_weights[slot], norm_gains[slot])
                    + source
                )

            def advance_unchanged(values, source):
                return values

            source = right_side[slot] if right_side is not None else jnp.zeros_like(before[slot])
            results.append(
                lax.cond(active[slot], advance_compute, advance_unchanged, before[slot], source)
            )
        return jnp.stack(results)

    def relaxation(current, level_index, residues, right_side, anchor):
        modulus = 4 * spacings[level_index]
        for residue in residues:
            before = incoming(current, level_index, anchor)
            active = points % modulus == residue
            current = jnp.where(
                shaped(active, 3), advance(before, level_index, active, right_side), current
            )
        return (current, None)

    def restrict(current, level_index, right_side, anchor):
        spacing = spacings[level_index]
        factor = float(spacing)
        wide_factor = float(4 * spacing)
        before = incoming(current, level_index, anchor)
        far_state = incoming(current, level_index + 1, anchor)
        active = points % (4 * spacing) == 0
        row_count = current.shape[1]
        coarse_list = []
        gap_list = []
        step_list = []
        for slot in range(slot_count):

            def restrict_compute(near, distant, held, source, slot=slot):
                update = branch(
                    jnp.concatenate([near, distant], axis=0),
                    first_weights[slot],
                    second_weights[slot],
                    norm_gains[slot],
                )
                near_term = update[:row_count]
                fine_value = near + factor * near_term + source
                coarse = fine_value - (distant + wide_factor * update[row_count:])
                gap = fine_value - held
                return (coarse, jnp.sum(gap * gap), jnp.sum(near_term * near_term))

            def restrict_unchanged(near, distant, held, source):
                nothing = jnp.zeros((), near.dtype)
                return (jnp.zeros_like(near), nothing, nothing)

            source = right_side[slot] if right_side is not None else jnp.zeros_like(before[slot])
            coarse, gap_sum, step_sum = lax.cond(
                active[slot],
                restrict_compute,
                restrict_unchanged,
                before[slot],
                far_state[slot],
                current[slot],
                source,
            )
            coarse_list.append(coarse)
            gap_list.append(gap_sum)
            step_list.append(step_sum)
        return (jnp.stack(coarse_list), jnp.stack(gap_list), jnp.stack(step_list))

    def defects(current, level_index, anchor):
        spacing = spacings[level_index]
        factor = float(spacing)
        before = incoming(current, level_index, anchor)
        stepped = []
        for slot in range(slot_count):
            stepped.append(
                before[slot]
                + factor
                * branch(before[slot], first_weights[slot], second_weights[slot], norm_gains[slot])
            )
        valid = shaped(points >= spacing, 3)
        return jnp.where(valid, current - jnp.stack(stepped), 0.0)

    def multigrid_cycle(anchor):
        current = jnp.broadcast_to(anchor, (slot_count,) + anchor.shape)
        current, unused = relaxation(current, 0, (1, 2, 3), None, anchor)
        current, unused = relaxation(current, 0, (0,), None, anchor)
        current, carried = relaxation(current, 0, (1, 2, 3), None, anchor)
        rhs_one, gap_sums, step_sums = restrict(current, 0, None, anchor)
        current, carried = relaxation(current, 1, (4, 8, 12), rhs_one, anchor)
        rhs_two, unused_gaps, unused_steps = restrict(current, 1, rhs_one, anchor)
        for coarse_step in range(1, layer_total // 16 + 1):
            active = points == 16 * coarse_step
            before = incoming(current, 2, anchor)
            current = jnp.where(shaped(active, 3), advance(before, 2, active, rhs_two), current)
        current, unused = relaxation(current, 1, (4, 8, 12), rhs_one, anchor)
        current, unused = relaxation(current, 0, (1, 2, 3), None, anchor)
        defects_four = defects(current, 1, anchor)
        defects_sixteen = defects(current, 2, anchor)
        return (current, gap_sums, step_sums, defects_four, defects_sixteen)

    portions = [initial]
    outcomes = [multigrid_cycle(portion) for portion in portions]
    layer_states = jnp.concatenate([outcome[0] for outcome in outcomes], axis=1)
    defects_four = jnp.concatenate([outcome[3] for outcome in outcomes], axis=1)
    defects_sixteen = jnp.concatenate([outcome[4] for outcome in outcomes], axis=1)
    gap_sums = outcomes[0][1]
    step_sums = outcomes[0][2]
    counted = (points % 4 == 0) & (points >= 8)
    entry_index = points // 4 - 2
    one_hot = (
        (jnp.arange(norm_count, dtype=jnp.int32)[None, :] == entry_index[:, None])
        & counted[:, None]
    ).astype(jnp.float32)
    gap_vector = jnp.sum(gap_sums[:, None] * one_hot, axis=0)
    step_vector = jnp.sum(step_sums[:, None] * one_hot, axis=0)
    gap_total, step_total = lax.psum((gap_vector, step_vector), ("layer", "dp"))
    residual_ratios = jnp.sqrt(gap_total / (step_total + epsilon))
    return (layer_states, residual_ratios, defects_four, defects_sixteen)


def local_quads(initial, norm_gains, first_weights, second_weights):
    sections = lax.axis_size("layer")
    blocks = sections // 4
    here = lax.axis_index("layer")
    place = here % 4
    rows = initial.shape[0]

    def moved(slot, *states):
        stacked = states[0] if len(states) == 1 else jnp.concatenate(states, axis=0)
        return branch(stacked, first_weights[slot], second_weights[slot], norm_gains[slot])

    def near(values):
        return jnp.where(here == 0, initial, shifted(values, "layer", 1))

    def distant(values):
        return jnp.where(here == 3, initial, shifted(values, "layer", 4))

    state = initial
    for slot in range(4):
        state = state + moved(slot, state)
    point = state
    left = near(point)
    far = distant(point)
    state = left
    for slot in range(3):
        state = state + moved(slot, state)
    update = moved(3, state, left, far)
    near_term = update[:rows]
    fine = state + near_term
    rhs_one = fine - (left + 4.0 * update[rows : 2 * rows])
    far_step = far + 16.0 * update[2 * rows :]
    gap = fine - point
    gap_sum = jnp.sum(gap * gap)
    step_sum = jnp.sum(near_term * near_term)
    point = jnp.where(place == 0, fine, point)
    for residue in (1, 2, 3):
        before = near(point)
        stepped = before + 4.0 * moved(3, before) + rhs_one
        point = jnp.where(place == residue, stepped, point)
    rhs_two = point - far_step
    wide = place == 3
    factor = jnp.where(wide, 16.0, 4.0)
    source = jnp.where(wide, rhs_two, rhs_one)
    for block in range(1, blocks):
        before = jnp.where(wide, distant(point), near(point))
        stepped = before + factor * moved(3, before) + source
        point = jnp.where((here == 4 * block) | (here == 4 * block + 3), stepped, point)
    for residue in (1, 2):
        before = near(point)
        stepped = before + 4.0 * moved(3, before) + rhs_one
        point = jnp.where(place == residue, stepped, point)
    left = near(point)
    far = distant(point)
    state = left
    states = []
    for slot in range(3):
        state = state + moved(slot, state)
        states.append(state)
    states.append(point)
    lefts = [shifted(s, "layer", 1) for s in states[:3]] + [left]
    fars = [shifted(s, "layer", 4) for s in states[:3]] + [far]
    fours = []
    sixteens = []
    for slot in range(4):
        update = moved(slot, lefts[slot], fars[slot])
        fours.append(states[slot] - (lefts[slot] + 4.0 * update[:rows]))
        sixteens.append(states[slot] - (fars[slot] + 16.0 * update[rows:]))
    points = here * 4 + jnp.arange(4, dtype=jnp.int32) + 1
    defects_four = jnp.where((points >= 4)[:, None, None], jnp.stack(fours), 0.0)
    defects_sixteen = jnp.where((points >= 16)[:, None, None], jnp.stack(sixteens), 0.0)
    one_hot = (jnp.arange(sections - 1) == here - 1).astype(jnp.float32)
    gap_total, step_total = lax.psum((gap_sum * one_hot, step_sum * one_hot), ("layer", "dp"))
    ratios = jnp.sqrt(gap_total / (step_total + epsilon))
    return (jnp.stack(states), ratios, defects_four, defects_sixteen)


def chosen(initial, norm_gains, first_weights, second_weights):
    quads = first_weights.shape[0] == 4 and lax.axis_size("layer") % 4 == 0
    return (local_quads if quads else local)(initial, norm_gains, first_weights, second_weights)


def solution(mesh):
    placed = (P("dp", None), P("layer", None), P("layer", None, None), P("layer", None, None))
    return jax.shard_map(
        chosen,
        mesh=mesh,
        in_specs=placed,
        out_specs=(P("layer", "dp", None), P(), P("layer", "dp", None), P("layer", "dp", None)),
        check_vma=False,
    )
```

profile of v0, /device:TPU:0, one launch (start us, length us, event | category | flops | bytes accessed | tf_op | source)
XLA Modules:
  0.0 269.5 jit_solution(11445225732891216298)
XLA Ops:
  2.6 5.4 %multiply_reduce_fusion.21 = (f32[64]{0:T(128)S(1)}, f32[64,1024]{1,0:T(8,128)S(1)}) fusion(f32[64,1024]{1,0:T(8,128)} %param.4, bf16[4,2048,1024]{2,1,0:T(8,128)(2,1)} %param.7, bf16[4,1024,2048]{2,1,0:T(8,128)(2,1)} %param.6, f32[1024]{0:T(1024)S(1)} %bitcast.351, f32[64]{0:T(128)S(1)} %add_rsqrt_fusion.20), kind=kOutput, calls=%fused_computation.443 | convolution fusion | flops 538443712 | bytes 9179648 | tf_op jit(solution)/shard_map/dot_general | solution.py:21
  8.0 5.4 %multiply_reduce_fusion.20 = (f32[64]{0:T(128)S(1)}, f32[64,1024]{1,0:T(8,128)S(1)}) fusion(f32[64,1024]{1,0:T(8,128)S(1)} %get-tuple-element.33, bf16[4,2048,1024]{2,1,0:T(8,128)(2,1)} %param.7, bf16[4,1024,2048]{2,1,0:T(8,128)(2,1)} %param.6, f32[1024]{0:T(1024)S(1)} %bitcast.338, f32[64]{0:T(128)S(1)} %add_rsqrt_fusion.19), kind=kOutput, calls=%fused_computation.441 | convolution fusion | flops 538443712 | bytes 9179904 | tf_op jit(solution)/shard_map/dot_general | solution.py:21
  13.4 5.3 %multiply_reduce_fusion.19 = (f32[64]{0:T(128)S(1)}, f32[64,1024]{1,0:T(8,128)S(1)}) fusion(f32[64,1024]{1,0:T(8,128)S(1)} %get-tuple-element.35, bf16[4,2048,1024]{2,1,0:T(8,128)(2,1)} %param.7, bf16[4,1024,2048]{2,1,0:T(8,128)(2,1)} %param.6, f32[1024]{0:T(1024)S(1)} %bitcast.334, f32[64]{0:T(128)S(1)} %add_rsqrt_fusion.18), kind=kOutput, calls=%fused_computation.439 | convolution fusion | flops 538443712 | bytes 9179904 | tf_op jit(solution)/shard_map/dot_general | solution.py:21
  18.8 5.2 %fusion.120 = f32[64,1024]{1,0:T(8,128)S(1)} fusion(f32[64,1024]{1,0:T(8,128)S(1)} %get-tuple-element.37, bf16[4,2048,1024]{2,1,0:T(8,128)(2,1)} %param.7, bf16[4,1024,2048]{2,1,0:T(8,128)(2,1)} %param.6, f32[1024]{0:T(1024)S(1)} %bitcast.342, f32[64]{0:T(128)S(1)} %add_rsqrt_fusion.17), kind=kOutput, calls=%fused_computation.121 | convolution fusion | flops 538312704 | bytes 9179648 | tf_op jit(solution)/shard_map/dot_general | solution.py:21
  24.0 4.9 %collective-permute-start.1 = (f32[64,1024]{1,0:T(8,128)S(1)}, f32[64,1024]{1,0:T(8,128)S(1)}, u32[]{:S(2)}, u32[]{:S(2)}) collective-permute-start(f32[64,1024]{1,0:T(8,128)S(1)} %fusion.120), channel_id=1, source_target_pairs={{0,16},{4,20},{8,24},{12,28},{1,17},{5,21},{9,25},{13,29},{2,18},{... | collective-permute-start | bytes 786440 | tf_op jit(solution)/shard_map/ppermute | solution.py:12
  28.9 1.7 collective-permute-start
  30.6 6.7 %collective-permute-done.1 = f32[64,1024]{1,0:T(8,128)S(1)} collective-permute-done((f32[64,1024]{1,0:T(8,128)S(1)}, f32[64,1024]{1,0:T(8,128)S(1)}, u32[]{:S(2)}, u32[]{:S(2)}) %collective-permute-start.1) | collective-permute-done | bytes 262176 | tf_op jit(solution)/shard_map/ppermute | solution.py:12
  37.4 5.3 %multiply_reduce_fusion.17 = (f32[64]{0:T(128)S(1)}, f32[64,1024]{1,0:T(8,128)S(1)}) fusion(f32[64,1024]{1,0:T(8,128)S(1)} %get-tuple-element.13, bf16[4,2048,1024]{2,1,0:T(8,128)(2,1)} %param.7, bf16[4,1024,2048]{2,1,0:T(8,128)(2,1)} %param.6, f32[64]{0:T(128)S(1)} %add_rsqrt_fusion.16, f32[1024]{0:T(1024)S(1)} %bitcast.352), kind=kOutput, calls=%fused_computation.435 | convolution fusion | flops 538443712 | bytes 9179904 | tf_op jit(solution)/shard_map/dot_general | solution.py:21
  42.7 5.3 %multiply_reduce_fusion.16 = (f32[64]{0:T(128)S(1)}, f32[64,1024]{1,0:T(8,128)S(1)}) fusion(f32[64,1024]{1,0:T(8,128)S(1)} %get-tuple-element.39, bf16[4,2048,1024]{2,1,0:T(8,128)(2,1)} %param.7, bf16[4,1024,2048]{2,1,0:T(8,128)(2,1)} %param.6, f32[64]{0:T(128)S(1)} %add_rsqrt_fusion.15, f32[1024]{0:T(1024)S(1)} %bitcast.339), kind=kOutput, calls=%fused_computation.433 | convolution fusion | flops 538443712 | bytes 9179904 | tf_op jit(solution)/shard_map/dot_general | solution.py:21
  48.1 5.2 %fusion.216 = f32[64,1024]{1,0:T(8,128)S(1)} fusion(f32[64,1024]{1,0:T(8,128)S(1)} %get-tuple-element.41, bf16[4,2048,1024]{2,1,0:T(8,128)(2,1)} %param.7, bf16[4,1024,2048]{2,1,0:T(8,128)(2,1)} %param.6, f32[64]{0:T(128)S(1)} %add_rsqrt_fusion.14, f32[1024]{0:T(1024)S(1)} %bitcast.335), kind=kOutput, calls=%fused_computation.153 | convolution fusion | flops 538312704 | bytes 9179648 | tf_op jit(solution)/shard_map/dot_general | solution.py:21
  53.5 5.7 %fusion.14 = f32[192,1024]{1,0:T(8,128)S(1)} fusion(f32[64,1024]{1,0:T(8,128)S(1)} %get-tuple-element.27, f32[64,1024]{1,0:T(8,128)S(1)} %get-tuple-element.13, f32[64,1024]{1,0:T(8,128)S(1)} %fusion.216, f32[1024]{0:T(1024)S(1)} %bitcast.343, f32[192]{0:T(256)S(1)} %add_rsqrt_fusion, bf16[4,2048,1024]{2,1,0:T(8,128)(2,1)} %param.7, ...), kind=kOutput, calls=%fused_computation.14 | convolution fusion | flops 1615134720 | bytes 9966336 | tf_op jit(solution)/shard_map/dot_general | solution.py:21
  59.9 1.3 collective-permute-start.2
  62.4 5.2 %fusion.192 = f32[64,1024]{1,0:T(8,128)S(1)} fusion(f32[64,1024]{1,0:T(8,128)S(1)} %get-tuple-element.14, f32[64,1024]{1,0:T(8,128)S(1)} %get-tuple-element.15, bf16[4,2048,1024]{2,1,0:T(8,128)(2,1)} %param.7, bf16[4,1024,2048]{2,1,0:T(8,128)(2,1)} %param.6, f32[64]{0:T(128)S(1)} %add_rsqrt_fusion.13, f32[1024]{0:T(1024)S(1)} %bitcast.344, pred[]{:T(512)S(6)} %eq.46, ...), kind=kOutput, calls=%fused_computation.145 | convolution fusion | flops 538640384 | bytes 10229760 | tf_op jit(solution)/shard_map/dot_general | solution.py:21
  67.7 5.6 %collective-permute-start.3 = (f32[64,1024]{1,0:T(8,128)S(1)}, f32[64,1024]{1,0:T(8,128)S(1)}, u32[]{:S(2)}, u32[]{:S(2)}) collective-permute-start(f32[64,1024]{1,0:T(8,128)S(1)} %fusion.192), channel_id=1, source_target_pairs={{0,4},{4,8},{8,12},{12,16},{16,20},{20,24},{24,28},{1,5},{5,9},{9,... | collective-permute-start | bytes 786440 | tf_op jit(solution)/shard_map/ppermute | solution.py:12
  74.6 5.2 %fusion.189 = f32[64,1024]{1,0:T(8,128)S(1)} fusion(f32[64,1024]{1,0:T(8,128)S(1)} %fusion.192, f32[64,1024]{1,0:T(8,128)S(1)} %get-tuple-element.15, bf16[4,2048,1024]{2,1,0:T(8,128)(2,1)} %param.7, bf16[4,1024,2048]{2,1,0:T(8,128)(2,1)} %param.6, f32[64]{0:T(128)S(1)} %add_rsqrt_fusion.12, f32[1024]{0:T(1024)S(1)} %bitcast.345, pred[]{:T(512)S(6)} %eq.23, ...), kind=kOutput, calls=%fused_computation.144 | convolution fusion | flops 538640384 | bytes 10229760 | tf_op jit(solution)/shard_map/dot_general | solution.py:21
  79.8 6.6 %collective-permute-start.4 = (f32[64,1024]{1,0:T(8,128)S(1)}, f32[64,1024]{1,0:T(8,128)S(1)}, u32[]{:S(2)}, u32[]{:S(2)}) collective-permute-start(f32[64,1024]{1,0:T(8,128)S(1)} %fusion.189), channel_id=1, source_target_pairs={{0,4},{4,8},{8,12},{12,16},{16,20},{20,24},{24,28},{1,5},{5,9},{9,... | collective-permute-start | bytes 786440 | tf_op jit(solution)/shard_map/ppermute | solution.py:12
  87.6 5.2 %fusion.186 = f32[64,1024]{1,0:T(8,128)S(1)} fusion(f32[64,1024]{1,0:T(8,128)S(1)} %fusion.189, f32[64,1024]{1,0:T(8,128)S(1)} %get-tuple-element.15, bf16[4,2048,1024]{2,1,0:T(8,128)(2,1)} %param.7, bf16[4,1024,2048]{2,1,0:T(8,128)(2,1)} %param.6, f32[64]{0:T(128)S(1)} %add_rsqrt_fusion.11, f32[1024]{0:T(1024)S(1)} %bitcast.346, pred[]{:T(512)S(6)} %eq.49, ...), kind=kOutput, calls=%fused_computation.143 | convolution fusion | flops 538640384 | bytes 10229760 | tf_op jit(solution)/shard_map/dot_general | solution.py:21
  92.9 6.6 %collective-permute-start.6 = (f32[64,1024]{1,0:T(8,128)S(1)}, f32[64,1024]{1,0:T(8,128)S(1)}, u32[]{:S(2)}, u32[]{:S(2)}) collective-permute-start(f32[64,1024]{1,0:T(8,128)S(1)} %fusion.186), channel_id=1, source_target_pairs={{0,4},{4,8},{8,12},{12,16},{16,20},{20,24},{24,28},{1,5},{5,9},{9,... | collective-permute-start | bytes 786440 | tf_op jit(solution)/shard_map/ppermute | solution.py:12
  99.4 8.8 %collective-permute-start.5 = (f32[64,1024]{1,0:T(8,128)S(1)}, f32[64,1024]{1,0:T(8,128)S(1)}, u32[]{:S(2)}, u32[]{:S(2)}) collective-permute-start(f32[64,1024]{1,0:T(8,128)S(1)} %fusion.186), channel_id=1, source_target_pairs={{0,16},{4,20},{8,24},{12,28},{1,17},{5,21},{9,25},{13,29},{2,18},{... | collective-permute-start | bytes 786440 | tf_op jit(solution)/shard_map/ppermute | solution.py:12
  108.3 4.8 %collective-permute-done.5 = f32[64,1024]{1,0:T(8,128)S(1)} collective-permute-done((f32[64,1024]{1,0:T(8,128)S(1)}, f32[64,1024]{1,0:T(8,128)S(1)}, u32[]{:S(2)}, u32[]{:S(2)}) %collective-permute-start.5) | collective-permute-done | bytes 262176 | tf_op jit(solution)/shard_map/ppermute | solution.py:12
  113.3 5.3 %fusion.183 = f32[64,1024]{1,0:T(8,128)S(1)} fusion(f32[64,1024]{1,0:T(8,128)S(1)} %fusion.186, f32[64,1024]{1,0:T(8,128)S(1)} %get-tuple-element.11, f32[64,1024]{1,0:T(8,128)S(1)} %get-tuple-element.15, f32[64,1024]{1,0:T(8,128)S(1)} %get-tuple-element.27, f32[192,1024]{1,0:T(8,128)S(1)} %fusion.14, bf16[4,2048,1024]{2,1,0:T(8,128)(2,1)} %param.7, ...), kind=kOutput, calls=%fused_computation.142 | convolution fusion | flops 538771456 | bytes 10228230 | tf_op jit(solution)/shard_map/dot_general | solution.py:21
  118.5 1.3 collective-permute-start.7
  119.8 1.1 collective-permute-done.7
  121.1 5.2 %fusion.180 = f32[64,1024]{1,0:T(8,128)S(1)} fusion(f32[64,1024]{1,0:T(8,128)S(1)} %fusion.183, f32[64,1024]{1,0:T(8,128)S(1)} %get-tuple-element.15, bf16[4,2048,1024]{2,1,0:T(8,128)(2,1)} %param.7, bf16[4,1024,2048]{2,1,0:T(8,128)(2,1)} %param.6, f32[64]{0:T(128)S(1)} %add_rsqrt_fusion.9, f32[1024]{0:T(1024)S(1)} %bitcast.348, pred[]{:T(512)S(6)} %eq.46, ...), kind=kOutput, calls=%fused_computation.141 | convolution fusion | flops 538640384 | bytes 10229760 | tf_op jit(solution)/shard_map/dot_general | solution.py:21
  126.3 2.3 collective-permute-start.8
  129.9 5.2 %fusion.177 = f32[64,1024]{1,0:T(8,128)S(1)} fusion(f32[64,1024]{1,0:T(8,128)S(1)} %fusion.180, f32[64,1024]{1,0:T(8,128)S(1)} %get-tuple-element.15, bf16[4,2048,1024]{2,1,0:T(8,128)(2,1)} %param.7, bf16[4,1024,2048]{2,1,0:T(8,128)(2,1)} %param.6, f32[64]{0:T(128)S(1)} %add_rsqrt_fusion.8, f32[1024]{0:T(1024)S(1)} %bitcast.349, pred[]{:T(512)S(6)} %eq.23, ...), kind=kOutput, calls=%fused_computation.140 | convolution fusion | flops 538640384 | bytes 10229760 | tf_op jit(solution)/shard_map/dot_general | solution.py:21
  135.1 15.7 %collective-permute-start.16 = (f32[64,1024]{1,0:T(8,128)S(1)}, f32[64,1024]{1,0:T(8,128)S(1)}, u32[]{:S(2)}, u32[]{:S(2)}) collective-permute-start(f32[64,1024]{1,0:T(8,128)S(1)} %fusion.177), channel_id=1, source_target_pairs={{0,16},{4,20},{8,24},{12,28},{1,17},{5,21},{9,25},{13,29},{2,18},{... | collective-permute-start | bytes 786440 | tf_op jit(solution)/shard_map/ppermute | solution.py:12
  150.9 1.3 collective-permute-start.9
  152.2 1.3 compare_select_fusion
  153.5 39.5 %all-reduce = (f32[7]{0:T(128)S(1)}, f32[7]{0:T(128)S(1)}) all-reduce(f32[7]{0:T(128)S(1)} %get-tuple-element.43, f32[7]{0:T(128)S(1)} %get-tuple-element.42), channel_id=1, replica_groups=mesh['layer'=8,'dp'=4] {'layer','dp'}, use_global_device_ids=true, to_apply=%region_18.19 | all-reduce | flops 14 | bytes 112 | tf_op jit(solution)/shard_map/psum | solution.py:259
  193.2 5.2 %fusion.201 = f32[64,1024]{1,0:T(8,128)S(1)} fusion(f32[64,1024]{1,0:T(8,128)S(1)} %get-tuple-element.9, bf16[4,2048,1024]{2,1,0:T(8,128)(2,1)} %param.7, bf16[4,1024,2048]{2,1,0:T(8,128)(2,1)} %param.6, f32[64]{0:T(128)S(1)} %add_rsqrt_fusion.7, f32[1024]{0:T(1024)S(1)} %bitcast.353), kind=kOutput, calls=%fused_computation.148 | convolution fusion | flops 538312704 | bytes 9179648 | tf_op jit(solution)/shard_map/dot_general | solution.py:21
  198.4 1.3 collective-permute-start.10
  200.3 4.8 %collective-permute-start.11 = (f32[64,1024]{1,0:T(8,128)S(1)}, f32[64,1024]{1,0:T(8,128)S(1)}, u32[]{:S(2)}, u32[]{:S(2)}) collective-permute-start(f32[64,1024]{1,0:T(8,128)S(1)} %fusion.201), channel_id=1, source_target_pairs={{0,16},{4,20},{8,24},{12,28},{1,17},{5,21},{9,25},{13,29},{2,18},{... | collective-permute-start | bytes 786440 | tf_op jit(solution)/shard_map/ppermute | solution.py:12
  205.2 7.2 %collective-permute-done.11 = f32[64,1024]{1,0:T(8,128)S(1)} collective-permute-done((f32[64,1024]{1,0:T(8,128)S(1)}, f32[64,1024]{1,0:T(8,128)S(1)}, u32[]{:S(2)}, u32[]{:S(2)}) %collective-permute-start.11) | collective-permute-done | bytes 262176 | tf_op jit(solution)/shard_map/ppermute | solution.py:12
  212.6 5.1 %fusion.68 = f32[128,1024]{1,0:T(8,128)S(1)} fusion(bf16[4,2048,1024]{2,1,0:T(8,128)(2,1)} %param.7, bf16[4,1024,2048]{2,1,0:T(8,128)(2,1)} %param.6, f32[128,1024]{1,0:T(8,128)S(1)} %constant_dynamic-update-slice_fusion, f32[1024]{0:T(1024)S(1)} %bitcast.354, f32[128]{0:T(128)S(1)} %add_rsqrt_fusion.4), kind=kOutput, calls=%fused_computation.68 | convolution fusion | flops 1076494336 | bytes 9441792 | tf_op jit(solution)/shard_map/dot_general | solution.py:21
  217.8 5.2 %fusion.210 = f32[64,1024]{1,0:T(8,128)S(1)} fusion(f32[64,1024]{1,0:T(8,128)S(1)} %fusion.201, bf16[4,2048,1024]{2,1,0:T(8,128)(2,1)} %param.7, bf16[4,1024,2048]{2,1,0:T(8,128)(2,1)} %param.6, f32[64]{0:T(128)S(1)} %add_rsqrt_fusion.6, f32[1024]{0:T(1024)S(1)} %bitcast.340), kind=kOutput, calls=%fused_computation.151 | convolution fusion | flops 538312704 | bytes 9179648 | tf_op jit(solution)/shard_map/dot_general | solution.py:21
  223.0 2.0 collective-permute-start.12
  225.0 4.7 %collective-permute-start.13 = (f32[64,1024]{1,0:T(8,128)S(1)}, f32[64,1024]{1,0:T(8,128)S(1)}, u32[]{:S(2)}, u32[]{:S(2)}) collective-permute-start(f32[64,1024]{1,0:T(8,128)S(1)} %fusion.210), channel_id=1, source_target_pairs={{0,16},{4,20},{8,24},{12,28},{1,17},{5,21},{9,25},{13,29},{2,18},{... | collective-permute-start | bytes 786440 | tf_op jit(solution)/shard_map/ppermute | solution.py:12
  229.7 5.8 %fusion = f32[128,1024]{1,0:T(8,128)} fusion(f32[64,1024]{1,0:T(8,128)S(1)} %get-tuple-element.26, f32[64,1024]{1,0:T(8,128)S(1)} %get-tuple-element.9, f32[1024]{0:T(1024)S(1)} %bitcast.350, f32[128]{0:T(128)S(1)} %add_rsqrt_fusion.1, bf16[4,2048,1024]{2,1,0:T(8,128)(2,1)} %param.7, bf16[4,1024,2048]{2,1,0:T(8,128)(2,1)} %param.6), kind=kOutput, calls=%fused_computation | convolution fusion | flops 1076625408 | bytes 9441792 | tf_op jit(solution)/shard_map/dot_general | solution.py:21
  235.5 1.7 collective-permute-done.13
  237.4 5.0 %fusion.52 = f32[128,1024]{1,0:T(8,128)S(1)} fusion(bf16[4,2048,1024]{2,1,0:T(8,128)(2,1)} %param.7, bf16[4,1024,2048]{2,1,0:T(8,128)(2,1)} %param.6, f32[128,1024]{1,0:T(8,128)S(1)} %constant_dynamic-update-slice_fusion.2, f32[1024]{0:T(1024)S(1)} %bitcast.341, f32[128]{0:T(128)S(1)} %add_rsqrt_fusion.3), kind=kOutput, calls=%fused_computation.52 | convolution fusion | flops 1076494336 | bytes 9441792 | tf_op jit(solution)/shard_map/dot_general | solution.py:21
  242.6 5.2 %fusion.219 = f32[64,1024]{1,0:T(8,128)S(1)} fusion(f32[64,1024]{1,0:T(8,128)S(1)} %fusion.210, bf16[4,2048,1024]{2,1,0:T(8,128)(2,1)} %param.7, bf16[4,1024,2048]{2,1,0:T(8,128)(2,1)} %param.6, f32[64]{0:T(128)S(1)} %add_rsqrt_fusion.5, f32[1024]{0:T(1024)S(1)} %bitcast.336), kind=kOutput, calls=%fused_computation.154 | convolution fusion | flops 538312704 | bytes 9179648 | tf_op jit(solution)/shard_map/dot_general | solution.py:21
  247.8 4.4 %collective-permute-start.15 = (f32[64,1024]{1,0:T(8,128)S(1)}, f32[64,1024]{1,0:T(8,128)S(1)}, u32[]{:S(2)}, u32[]{:S(2)}) collective-permute-start(f32[64,1024]{1,0:T(8,128)S(1)} %fusion.219), channel_id=1, source_target_pairs={{0,16},{4,20},{8,24},{12,28},{1,17},{5,21},{9,25},{13,29},{2,18},{... | collective-permute-start | bytes 786440 | tf_op jit(solution)/shard_map/ppermute | solution.py:12
  252.3 1.7 collective-permute-start.14
  255.0 2.0 pad_maximum_fusion
  257.1 3.7 %collective-permute-done.15 = f32[64,1024]{1,0:T(8,128)S(1)} collective-permute-done((f32[64,1024]{1,0:T(8,128)S(1)}, f32[64,1024]{1,0:T(8,128)S(1)}, u32[]{:S(2)}, u32[]{:S(2)}) %collective-permute-start.15) | collective-permute-done | bytes 262176 | tf_op jit(solution)/shard_map/ppermute | solution.py:12
  260.9 5.9 %fusion.36 = f32[128,1024]{1,0:T(8,128)} fusion(bf16[4,2048,1024]{2,1,0:T(8,128)(2,1)} %param.7, bf16[4,1024,2048]{2,1,0:T(8,128)(2,1)} %param.6, f32[128,1024]{1,0:T(8,128)S(1)} %constant_dynamic-update-slice_fusion.4, f32[1024]{0:T(1024)S(1)} %bitcast.337, f32[128]{0:T(128)S(1)} %add_rsqrt_fusion.2), kind=kOutput, calls=%fused_computation.36 | convolution fusion | flops 1076494336 | bytes 9441792 | tf_op jit(solution)/shard_map/dot_general | solution.py:21
  267.9 1.6 maximum_select_fusion
  (65 shorter events, 12.2 us)
Async XLA Ops:
  8.0 29.2 %copy-start = (f32[64,1024]{1,0:T(8,128)S(1)}, f32[64,1024]{1,0:T(8,128)}, u32[]{:S(2)}) copy-start(f32[64,1024]{1,0:T(8,128)} %param.4) | copy-start | bytes 786436
  24.0 13.3 %collective-permute-start.1 = (f32[64,1024]{1,0:T(8,128)S(1)}, f32[64,1024]{1,0:T(8,128)S(1)}, u32[]{:S(2)}, u32[]{:S(2)}) collective-permute-start(f32[64,1024]{1,0:T(8,128)S(1)} %fusion.120), channel_id=1, source_target_pairs={{0,16},{4,20},{8,24},{12,28},{1,17},{5,21},{9,25},{13,29},{2,18},{... | collective-permute-start | bytes 786440 | tf_op jit(solution)/shard_map/ppermute | solution.py:12
  28.9 8.3 %collective-permute-start = (f32[64,1024]{1,0:T(8,128)S(1)}, f32[64,1024]{1,0:T(8,128)S(1)}, u32[]{:S(2)}, u32[]{:S(2)}) collective-permute-start(f32[64,1024]{1,0:T(8,128)S(1)} %fusion.120), channel_id=1, source_target_pairs={{0,4},{4,8},{8,12},{12,16},{16,20},{20,24},{24,28},{1,5},{5,9},{9,... | collective-permute-start | bytes 786440 | tf_op jit(solution)/shard_map/ppermute | solution.py:12
  59.9 2.4 collective-permute-start.2
  67.7 6.8 %collective-permute-start.3 = (f32[64,1024]{1,0:T(8,128)S(1)}, f32[64,1024]{1,0:T(8,128)S(1)}, u32[]{:S(2)}, u32[]{:S(2)}) collective-permute-start(f32[64,1024]{1,0:T(8,128)S(1)} %fusion.192), channel_id=1, source_target_pairs={{0,4},{4,8},{8,12},{12,16},{16,20},{20,24},{24,28},{1,5},{5,9},{9,... | collective-permute-start | bytes 786440 | tf_op jit(solution)/shard_map/ppermute | solution.py:12
  79.8 7.7 %collective-permute-start.4 = (f32[64,1024]{1,0:T(8,128)S(1)}, f32[64,1024]{1,0:T(8,128)S(1)}, u32[]{:S(2)}, u32[]{:S(2)}) collective-permute-start(f32[64,1024]{1,0:T(8,128)S(1)} %fusion.189), channel_id=1, source_target_pairs={{0,4},{4,8},{8,12},{12,16},{16,20},{20,24},{24,28},{1,5},{5,9},{9,... | collective-permute-start | bytes 786440 | tf_op jit(solution)/shard_map/ppermute | solution.py:12
  92.9 15.4 %collective-permute-start.6 = (f32[64,1024]{1,0:T(8,128)S(1)}, f32[64,1024]{1,0:T(8,128)S(1)}, u32[]{:S(2)}, u32[]{:S(2)}) collective-permute-start(f32[64,1024]{1,0:T(8,128)S(1)} %fusion.186), channel_id=1, source_target_pairs={{0,4},{4,8},{8,12},{12,16},{16,20},{20,24},{24,28},{1,5},{5,9},{9,... | collective-permute-start | bytes 786440 | tf_op jit(solution)/shard_map/ppermute | solution.py:12
  99.4 13.7 %collective-permute-start.5 = (f32[64,1024]{1,0:T(8,128)S(1)}, f32[64,1024]{1,0:T(8,128)S(1)}, u32[]{:S(2)}, u32[]{:S(2)}) collective-permute-start(f32[64,1024]{1,0:T(8,128)S(1)} %fusion.186), channel_id=1, source_target_pairs={{0,16},{4,20},{8,24},{12,28},{1,17},{5,21},{9,25},{13,29},{2,18},{... | collective-permute-start | bytes 786440 | tf_op jit(solution)/shard_map/ppermute | solution.py:12
  118.5 2.4 collective-permute-start.7
  126.3 3.4 %collective-permute-start.8 = (f32[64,1024]{1,0:T(8,128)S(1)}, f32[64,1024]{1,0:T(8,128)S(1)}, u32[]{:S(2)}, u32[]{:S(2)}) collective-permute-start(f32[64,1024]{1,0:T(8,128)S(1)} %fusion.180), channel_id=1, source_target_pairs={{0,4},{4,8},{8,12},{12,16},{16,20},{20,24},{24,28},{1,5},{5,9},{9,... | collective-permute-start | bytes 786440 | tf_op jit(solution)/shard_map/ppermute | solution.py:12
  135.1 57.9 %collective-permute-start.16 = (f32[64,1024]{1,0:T(8,128)S(1)}, f32[64,1024]{1,0:T(8,128)S(1)}, u32[]{:S(2)}, u32[]{:S(2)}) collective-permute-start(f32[64,1024]{1,0:T(8,128)S(1)} %fusion.177), channel_id=1, source_target_pairs={{0,16},{4,20},{8,24},{12,28},{1,17},{5,21},{9,25},{13,29},{2,18},{... | collective-permute-start | bytes 786440 | tf_op jit(solution)/shard_map/ppermute | solution.py:12
  150.9 42.2 %collective-permute-start.9 = (f32[64,1024]{1,0:T(8,128)S(1)}, f32[64,1024]{1,0:T(8,128)S(1)}, u32[]{:S(2)}, u32[]{:S(2)}) collective-permute-start(f32[64,1024]{1,0:T(8,128)S(1)} %fusion.177), channel_id=1, source_target_pairs={{0,4},{4,8},{8,12},{12,16},{16,20},{20,24},{24,28},{1,5},{5,9},{9,... | collective-permute-start | bytes 786440 | tf_op jit(solution)/shard_map/ppermute | solution.py:12
  198.4 6.8 %collective-permute-start.10 = (f32[64,1024]{1,0:T(8,128)S(1)}, f32[64,1024]{1,0:T(8,128)S(1)}, u32[]{:S(2)}, u32[]{:S(2)}) collective-permute-start(f32[64,1024]{1,0:T(8,128)S(1)} %fusion.201), channel_id=1, source_target_pairs={{0,4},{4,8},{8,12},{12,16},{16,20},{20,24},{24,28},{1,5},{5,9},{9,... | collective-permute-start | bytes 786440 | tf_op jit(solution)/shard_map/ppermute | solution.py:12
  200.3 12.2 %collective-permute-start.11 = (f32[64,1024]{1,0:T(8,128)S(1)}, f32[64,1024]{1,0:T(8,128)S(1)}, u32[]{:S(2)}, u32[]{:S(2)}) collective-permute-start(f32[64,1024]{1,0:T(8,128)S(1)} %fusion.201), channel_id=1, source_target_pairs={{0,16},{4,20},{8,24},{12,28},{1,17},{5,21},{9,25},{13,29},{2,18},{... | collective-permute-start | bytes 786440 | tf_op jit(solution)/shard_map/ppermute | solution.py:12
  223.0 19.6 %copy-start.1 = (f32[64,1024]{1,0:T(8,128)}, f32[64,1024]{1,0:T(8,128)S(1)}, u32[]{:S(2)}) copy-start(f32[64,1024]{1,0:T(8,128)S(1)} %fusion.210) | copy-start | bytes 786436
  223.0 12.5 %collective-permute-start.12 = (f32[64,1024]{1,0:T(8,128)S(1)}, f32[64,1024]{1,0:T(8,128)S(1)}, u32[]{:S(2)}, u32[]{:S(2)}) collective-permute-start(f32[64,1024]{1,0:T(8,128)S(1)} %fusion.210), channel_id=1, source_target_pairs={{0,4},{4,8},{8,12},{12,16},{16,20},{20,24},{24,28},{1,5},{5,9},{9,... | collective-permute-start | bytes 786440 | tf_op jit(solution)/shard_map/ppermute | solution.py:12
  225.0 12.2 %collective-permute-start.13 = (f32[64,1024]{1,0:T(8,128)S(1)}, f32[64,1024]{1,0:T(8,128)S(1)}, u32[]{:S(2)}, u32[]{:S(2)}) collective-permute-start(f32[64,1024]{1,0:T(8,128)S(1)} %fusion.210), channel_id=1, source_target_pairs={{0,16},{4,20},{8,24},{12,28},{1,17},{5,21},{9,25},{13,29},{2,18},{... | collective-permute-start | bytes 786440 | tf_op jit(solution)/shard_map/ppermute | solution.py:12
  247.8 12.9 %collective-permute-start.15 = (f32[64,1024]{1,0:T(8,128)S(1)}, f32[64,1024]{1,0:T(8,128)S(1)}, u32[]{:S(2)}, u32[]{:S(2)}) collective-permute-start(f32[64,1024]{1,0:T(8,128)S(1)} %fusion.219), channel_id=1, source_target_pairs={{0,16},{4,20},{8,24},{12,28},{1,17},{5,21},{9,25},{13,29},{2,18},{... | collective-permute-start | bytes 786440 | tf_op jit(solution)/shard_map/ppermute | solution.py:12
  252.3 4.8 %collective-permute-start.14 = (f32[64,1024]{1,0:T(8,128)S(1)}, f32[64,1024]{1,0:T(8,128)S(1)}, u32[]{:S(2)}, u32[]{:S(2)}) collective-permute-start(f32[64,1024]{1,0:T(8,128)S(1)} %fusion.219), channel_id=1, source_target_pairs={{0,4},{4,8},{8,12},{12,16},{16,20},{20,24},{24,28},{1,5},{5,9},{9,... | collective-permute-start | bytes 786440 | tf_op jit(solution)/shard_map/ppermute | solution.py:12
where the time goes:
time: 270 us; the launch traced here: 269 us
  matrix products  112 us (41%)
  starting transfers between devices  74.9 us (28%)
  blocking collectives  39.5 us (15%)
  waiting for transfers between devices  29.7 us (11%)
  other arithmetic  11.6 us (4%)
    dot_general x21, matrix products, branch(): return jnp.dot(hidden, weight_out, preferred_element_type=jnp.float32)  112 us
    ppermute x17, starting transfers between devices, shifted(): return lax.ppermute(block, axis, route)  74.9 us
    psum x1, blocking collectives, local_quads(): lax.psum((gap_sum * one_hot, step_sum * one_hot), ('layer', 'dp'))  39.5 us
    ppermute x17, waiting for transfers between devices, shifted(): return lax.ppermute(block, axis, route)  29.7 us
  transfers between devices with their start and end apart: 17, of which 10 were waited for; matrix products, arithmetic and copies ran while one was open for 4% of the time, Pallas kernels for 0%

commit v1 on v0

--- a/solution.py
+++ b/solution.py
@@ -256,7 +256,9 @@
     defects_four = jnp.where((points >= 4)[:, None, None], jnp.stack(fours), 0.0)
     defects_sixteen = jnp.where((points >= 16)[:, None, None], jnp.stack(sixteens), 0.0)
     one_hot = (jnp.arange(sections - 1) == here - 1).astype(jnp.float32)
-    gap_total, step_total = lax.psum((gap_sum * one_hot, step_sum * one_hot), ("layer", "dp"))
+    gap_total, step_total = lax.psum(
+        lax.psum((gap_sum * one_hot, step_sum * one_hot), "dp"), "layer"
+    )
     ratios = jnp.sqrt(gap_total / (step_total + epsilon))
     return (jnp.stack(states), ratios, defects_four, defects_sixteen)
 

time: 270 us -> 253 us (0.937)
  blocking collectives: 39.5 us -> 23.7 us
    psum x1 -> x2, blocking collectives: 39.5 us -> 23.7 us  [the longest x1 12 us: local_quads(): lax.psum((gap_sum * one_hot, step_sum * one_hot), 'dp')]
where the time goes in v1:
time: 253 us; the launch traced here: 252 us
  matrix products  112 us (44%)
  starting transfers between devices  73.1 us (29%)
  waiting for transfers between devices  29.8 us (12%)
  blocking collectives  23.7 us (9%)
  other arithmetic  11.6 us (5%)
    dot_general x21, matrix products, branch(): return jnp.dot(hidden, weight_out, preferred_element_type=jnp.float32)  112 us
    ppermute x17, starting transfers between devices, shifted(): return lax.ppermute(block, axis, route)  73.1 us
    ppermute x17, waiting for transfers between devices, shifted(): return lax.ppermute(block, axis, route)  29.8 us
    psum x1, blocking collectives, local_quads(): lax.psum((gap_sum * one_hot, step_sum * one_hot), 'dp')  12 us
    psum x1, blocking collectives, local_quads(): lax.psum(lax.psum((gap_sum * one_hot, step_sum * one_hot), 'dp'), 'layer')  11.8 us
  transfers between devices with their start and end apart: 17, of which 10 were waited for; matrix products, arithmetic and copies ran while one was open for 4% of the time, Pallas kernels for 0%

profile of v1, /device:TPU:0, one launch (start us, length us, event | category | flops | bytes accessed | tf_op | source)
XLA Modules:
  0.0 252.0 jit_solution(6070104555537408343)
XLA Ops:
  2.6 5.4 %multiply_reduce_fusion.21 = (f32[64]{0:T(128)S(1)}, f32[64,1024]{1,0:T(8,128)S(1)}) fusion(f32[64,1024]{1,0:T(8,128)} %param.4, bf16[4,2048,1024]{2,1,0:T(8,128)(2,1)} %param.7, bf16[4,1024,2048]{2,1,0:T(8,128)(2,1)} %param.6, f32[1024]{0:T(1024)S(1)} %bitcast.351, f32[64]{0:T(128)S(1)} %add_rsqrt_fusion.20), kind=kOutput, calls=%fused_computation.443 | convolution fusion | flops 538443712 | bytes 9179648 | tf_op jit(solution)/shard_map/dot_general | solution.py:21
  8.0 5.4 %multiply_reduce_fusion.20 = (f32[64]{0:T(128)S(1)}, f32[64,1024]{1,0:T(8,128)S(1)}) fusion(f32[64,1024]{1,0:T(8,128)S(1)} %get-tuple-element.35, bf16[4,2048,1024]{2,1,0:T(8,128)(2,1)} %param.7, bf16[4,1024,2048]{2,1,0:T(8,128)(2,1)} %param.6, f32[1024]{0:T(1024)S(1)} %bitcast.338, f32[64]{0:T(128)S(1)} %add_rsqrt_fusion.19), kind=kOutput, calls=%fused_computation.441 | convolution fusion | flops 538443712 | bytes 9179904 | tf_op jit(solution)/shard_map/dot_general | solution.py:21
  13.4 5.3 %multiply_reduce_fusion.19 = (f32[64]{0:T(128)S(1)}, f32[64,1024]{1,0:T(8,128)S(1)}) fusion(f32[64,1024]{1,0:T(8,128)S(1)} %get-tuple-element.37, bf16[4,2048,1024]{2,1,0:T(8,128)(2,1)} %param.7, bf16[4,1024,2048]{2,1,0:T(8,128)(2,1)} %param.6, f32[1024]{0:T(1024)S(1)} %bitcast.334, f32[64]{0:T(128)S(1)} %add_rsqrt_fusion.18), kind=kOutput, calls=%fused_computation.439 | convolution fusion | flops 538443712 | bytes 9179904 | tf_op jit(solution)/shard_map/dot_general | solution.py:21
  18.8 5.2 %fusion.120 = f32[64,1024]{1,0:T(8,128)S(1)} fusion(f32[64,1024]{1,0:T(8,128)S(1)} %get-tuple-element.39, bf16[4,2048,1024]{2,1,0:T(8,128)(2,1)} %param.7, bf16[4,1024,2048]{2,1,0:T(8,128)(2,1)} %param.6, f32[1024]{0:T(1024)S(1)} %bitcast.342, f32[64]{0:T(128)S(1)} %add_rsqrt_fusion.17), kind=kOutput, calls=%fused_computation.121 | convolution fusion | flops 538312704 | bytes 9179648 | tf_op jit(solution)/shard_map/dot_general | solution.py:21
  24.0 4.9 %collective-permute-start.1 = (f32[64,1024]{1,0:T(8,128)S(1)}, f32[64,1024]{1,0:T(8,128)S(1)}, u32[]{:S(2)}, u32[]{:S(2)}) collective-permute-start(f32[64,1024]{1,0:T(8,128)S(1)} %fusion.120), channel_id=1, source_target_pairs={{0,16},{4,20},{8,24},{12,28},{1,17},{5,21},{9,25},{13,29},{2,18},{... | collective-permute-start | bytes 786440 | tf_op jit(solution)/shard_map/ppermute | solution.py:12
  28.9 1.7 collective-permute-start
  30.6 6.7 %collective-permute-done.1 = f32[64,1024]{1,0:T(8,128)S(1)} collective-permute-done((f32[64,1024]{1,0:T(8,128)S(1)}, f32[64,1024]{1,0:T(8,128)S(1)}, u32[]{:S(2)}, u32[]{:S(2)}) %collective-permute-start.1) | collective-permute-done | bytes 262176 | tf_op jit(solution)/shard_map/ppermute | solution.py:12
  37.4 5.3 %multiply_reduce_fusion.17 = (f32[64]{0:T(128)S(1)}, f32[64,1024]{1,0:T(8,128)S(1)}) fusion(f32[64,1024]{1,0:T(8,128)S(1)} %get-tuple-element.15, bf16[4,2048,1024]{2,1,0:T(8,128)(2,1)} %param.7, bf16[4,1024,2048]{2,1,0:T(8,128)(2,1)} %param.6, f32[64]{0:T(128)S(1)} %add_rsqrt_fusion.16, f32[1024]{0:T(1024)S(1)} %bitcast.352), kind=kOutput, calls=%fused_computation.435 | convolution fusion | flops 538443712 | bytes 9179904 | tf_op jit(solution)/shard_map/dot_general | solution.py:21
  42.7 5.3 %multiply_reduce_fusion.16 = (f32[64]{0:T(128)S(1)}, f32[64,1024]{1,0:T(8,128)S(1)}) fusion(f32[64,1024]{1,0:T(8,128)S(1)} %get-tuple-element.41, bf16[4,2048,1024]{2,1,0:T(8,128)(2,1)} %param.7, bf16[4,1024,2048]{2,1,0:T(8,128)(2,1)} %param.6, f32[64]{0:T(128)S(1)} %add_rsqrt_fusion.15, f32[1024]{0:T(1024)S(1)} %bitcast.339), kind=kOutput, calls=%fused_computation.433 | convolution fusion | flops 538443712 | bytes 9179904 | tf_op jit(solution)/shard_map/dot_general | solution.py:21
  48.1 5.2 %fusion.216 = f32[64,1024]{1,0:T(8,128)S(1)} fusion(f32[64,1024]{1,0:T(8,128)S(1)} %get-tuple-element.43, bf16[4,2048,1024]{2,1,0:T(8,128)(2,1)} %param.7, bf16[4,1024,2048]{2,1,0:T(8,128)(2,1)} %param.6, f32[64]{0:T(128)S(1)} %add_rsqrt_fusion.14, f32[1024]{0:T(1024)S(1)} %bitcast.335), kind=kOutput, calls=%fused_computation.153 | convolution fusion | flops 538312704 | bytes 9179648 | tf_op jit(solution)/shard_map/dot_general | solution.py:21
  53.5 5.7 %fusion.14 = f32[192,1024]{1,0:T(8,128)S(1)} fusion(f32[64,1024]{1,0:T(8,128)S(1)} %get-tuple-element.29, f32[64,1024]{1,0:T(8,128)S(1)} %get-tuple-element.15, f32[64,1024]{1,0:T(8,128)S(1)} %fusion.216, f32[1024]{0:T(1024)S(1)} %bitcast.343, f32[192]{0:T(256)S(1)} %add_rsqrt_fusion, bf16[4,2048,1024]{2,1,0:T(8,128)(2,1)} %param.7, ...), kind=kOutput, calls=%fused_computation.14 | convolution fusion | flops 1615134720 | bytes 9966336 | tf_op jit(solution)/shard_map/dot_general | solution.py:21
  59.9 1.3 collective-permute-start.2
  62.4 5.2 %fusion.192 = f32[64,1024]{1,0:T(8,128)S(1)} fusion(f32[64,1024]{1,0:T(8,128)S(1)} %get-tuple-element.16, f32[64,1024]{1,0:T(8,128)S(1)} %get-tuple-element.17, bf16[4,2048,1024]{2,1,0:T(8,128)(2,1)} %param.7, bf16[4,1024,2048]{2,1,0:T(8,128)(2,1)} %param.6, f32[64]{0:T(128)S(1)} %add_rsqrt_fusion.13, f32[1024]{0:T(1024)S(1)} %bitcast.344, pred[]{:T(512)S(6)} %eq.46, ...), kind=kOutput, calls=%fused_computation.145 | convolution fusion | flops 538640384 | bytes 10229760 | tf_op jit(solution)/shard_map/dot_general | solution.py:21
  67.7 5.6 %collective-permute-start.3 = (f32[64,1024]{1,0:T(8,128)S(1)}, f32[64,1024]{1,0:T(8,128)S(1)}, u32[]{:S(2)}, u32[]{:S(2)}) collective-permute-start(f32[64,1024]{1,0:T(8,128)S(1)} %fusion.192), channel_id=1, source_target_pairs={{0,4},{4,8},{8,12},{12,16},{16,20},{20,24},{24,28},{1,5},{5,9},{9,... | collective-permute-start | bytes 786440 | tf_op jit(solution)/shard_map/ppermute | solution.py:12
  74.6 5.2 %fusion.189 = f32[64,1024]{1,0:T(8,128)S(1)} fusion(f32[64,1024]{1,0:T(8,128)S(1)} %fusion.192, f32[64,1024]{1,0:T(8,128)S(1)} %get-tuple-element.17, bf16[4,2048,1024]{2,1,0:T(8,128)(2,1)} %param.7, bf16[4,1024,2048]{2,1,0:T(8,128)(2,1)} %param.6, f32[64]{0:T(128)S(1)} %add_rsqrt_fusion.12, f32[1024]{0:T(1024)S(1)} %bitcast.345, pred[]{:T(512)S(6)} %eq.23, ...), kind=kOutput, calls=%fused_computation.144 | convolution fusion | flops 538640384 | bytes 10229760 | tf_op jit(solution)/shard_map/dot_general | solution.py:21
  79.8 6.6 %collective-permute-start.4 = (f32[64,1024]{1,0:T(8,128)S(1)}, f32[64,1024]{1,0:T(8,128)S(1)}, u32[]{:S(2)}, u32[]{:S(2)}) collective-permute-start(f32[64,1024]{1,0:T(8,128)S(1)} %fusion.189), channel_id=1, source_target_pairs={{0,4},{4,8},{8,12},{12,16},{16,20},{20,24},{24,28},{1,5},{5,9},{9,... | collective-permute-start | bytes 786440 | tf_op jit(solution)/shard_map/ppermute | solution.py:12
  87.6 5.2 %fusion.186 = f32[64,1024]{1,0:T(8,128)S(1)} fusion(f32[64,1024]{1,0:T(8,128)S(1)} %fusion.189, f32[64,1024]{1,0:T(8,128)S(1)} %get-tuple-element.17, bf16[4,2048,1024]{2,1,0:T(8,128)(2,1)} %param.7, bf16[4,1024,2048]{2,1,0:T(8,128)(2,1)} %param.6, f32[64]{0:T(128)S(1)} %add_rsqrt_fusion.11, f32[1024]{0:T(1024)S(1)} %bitcast.346, pred[]{:T(512)S(6)} %eq.49, ...), kind=kOutput, calls=%fused_computation.143 | convolution fusion | flops 538640384 | bytes 10229760 | tf_op jit(solution)/shard_map/dot_general | solution.py:21
  92.9 6.6 %collective-permute-start.6 = (f32[64,1024]{1,0:T(8,128)S(1)}, f32[64,1024]{1,0:T(8,128)S(1)}, u32[]{:S(2)}, u32[]{:S(2)}) collective-permute-start(f32[64,1024]{1,0:T(8,128)S(1)} %fusion.186), channel_id=1, source_target_pairs={{0,4},{4,8},{8,12},{12,16},{16,20},{20,24},{24,28},{1,5},{5,9},{9,... | collective-permute-start | bytes 786440 | tf_op jit(solution)/shard_map/ppermute | solution.py:12
  99.4 8.8 %collective-permute-start.5 = (f32[64,1024]{1,0:T(8,128)S(1)}, f32[64,1024]{1,0:T(8,128)S(1)}, u32[]{:S(2)}, u32[]{:S(2)}) collective-permute-start(f32[64,1024]{1,0:T(8,128)S(1)} %fusion.186), channel_id=1, source_target_pairs={{0,16},{4,20},{8,24},{12,28},{1,17},{5,21},{9,25},{13,29},{2,18},{... | collective-permute-start | bytes 786440 | tf_op jit(solution)/shard_map/ppermute | solution.py:12
  108.3 4.8 %collective-permute-done.5 = f32[64,1024]{1,0:T(8,128)S(1)} collective-permute-done((f32[64,1024]{1,0:T(8,128)S(1)}, f32[64,1024]{1,0:T(8,128)S(1)}, u32[]{:S(2)}, u32[]{:S(2)}) %collective-permute-start.5) | collective-permute-done | bytes 262176 | tf_op jit(solution)/shard_map/ppermute | solution.py:12
  113.3 5.3 %fusion.183 = f32[64,1024]{1,0:T(8,128)S(1)} fusion(f32[64,1024]{1,0:T(8,128)S(1)} %fusion.186, f32[64,1024]{1,0:T(8,128)S(1)} %get-tuple-element.13, f32[64,1024]{1,0:T(8,128)S(1)} %get-tuple-element.17, f32[64,1024]{1,0:T(8,128)S(1)} %get-tuple-element.29, f32[192,1024]{1,0:T(8,128)S(1)} %fusion.14, bf16[4,2048,1024]{2,1,0:T(8,128)(2,1)} %param.7, ...), kind=kOutput, calls=%fused_computation.142 | convolution fusion | flops 538771456 | bytes 10228230 | tf_op jit(solution)/shard_map/dot_general | solution.py:21
  118.5 1.3 collective-permute-start.7
  121.1 5.2 %fusion.180 = f32[64,1024]{1,0:T(8,128)S(1)} fusion(f32[64,1024]{1,0:T(8,128)S(1)} %fusion.183, f32[64,1024]{1,0:T(8,128)S(1)} %get-tuple-element.17, bf16[4,2048,1024]{2,1,0:T(8,128)(2,1)} %param.7, bf16[4,1024,2048]{2,1,0:T(8,128)(2,1)} %param.6, f32[64]{0:T(128)S(1)} %add_rsqrt_fusion.9, f32[1024]{0:T(1024)S(1)} %bitcast.348, pred[]{:T(512)S(6)} %eq.46, ...), kind=kOutput, calls=%fused_computation.141 | convolution fusion | flops 538640384 | bytes 10229760 | tf_op jit(solution)/shard_map/dot_general | solution.py:21
  126.3 2.3 collective-permute-start.8
  129.9 5.2 %fusion.177 = f32[64,1024]{1,0:T(8,128)S(1)} fusion(f32[64,1024]{1,0:T(8,128)S(1)} %fusion.180, f32[64,1024]{1,0:T(8,128)S(1)} %get-tuple-element.17, bf16[4,2048,1024]{2,1,0:T(8,128)(2,1)} %param.7, bf16[4,1024,2048]{2,1,0:T(8,128)(2,1)} %param.6, f32[64]{0:T(128)S(1)} %add_rsqrt_fusion.8, f32[1024]{0:T(1024)S(1)} %bitcast.349, pred[]{:T(512)S(6)} %eq.23, ...), kind=kOutput, calls=%fused_computation.140 | convolution fusion | flops 538640384 | bytes 10229760 | tf_op jit(solution)/shard_map/dot_general | solution.py:21
  135.1 15.7 %collective-permute-start.16 = (f32[64,1024]{1,0:T(8,128)S(1)}, f32[64,1024]{1,0:T(8,128)S(1)}, u32[]{:S(2)}, u32[]{:S(2)}) collective-permute-start(f32[64,1024]{1,0:T(8,128)S(1)} %fusion.177), channel_id=1, source_target_pairs={{0,16},{4,20},{8,24},{12,28},{1,17},{5,21},{9,25},{13,29},{2,18},{... | collective-permute-start | bytes 786440 | tf_op jit(solution)/shard_map/ppermute | solution.py:12
  150.9 1.3 collective-permute-start.9
  152.2 1.3 compare_select_fusion
  153.5 12.0 %all-reduce.1 = (f32[7]{0:T(128)S(1)}, f32[7]{0:T(128)S(1)}) all-reduce(f32[7]{0:T(128)S(1)} %get-tuple-element.45, f32[7]{0:T(128)S(1)} %get-tuple-element.44), channel_id=1, replica_groups=mesh['layer'=8,'dp'=4] {'dp'}, use_global_device_ids=true, to_apply=%region_18.19 | all-reduce | flops 14 | bytes 112 | tf_op jit(solution)/shard_map/psum | solution.py:260
  165.5 11.8 %all-reduce = (f32[7]{0:T(128)S(1)}, f32[7]{0:T(128)S(1)}) all-reduce(f32[7]{0:T(128)S(1)} %get-tuple-element.8, f32[7]{0:T(128)S(1)} %get-tuple-element.9), channel_id=1, replica_groups=mesh['layer'=8,'dp'=4] {'layer'}, use_global_device_ids=true, to_apply=%region_19.20 | all-reduce | flops 14 | bytes 112 | tf_op jit(solution)/shard_map/psum | solution.py:259
  177.4 5.2 %fusion.201 = f32[64,1024]{1,0:T(8,128)S(1)} fusion(f32[64,1024]{1,0:T(8,128)S(1)} %get-tuple-element.11, bf16[4,2048,1024]{2,1,0:T(8,128)(2,1)} %param.7, bf16[4,1024,2048]{2,1,0:T(8,128)(2,1)} %param.6, f32[64]{0:T(128)S(1)} %add_rsqrt_fusion.7, f32[1024]{0:T(1024)S(1)} %bitcast.353), kind=kOutput, calls=%fused_computation.148 | convolution fusion | flops 538312704 | bytes 9179648 | tf_op jit(solution)/shard_map/dot_general | solution.py:21
  182.6 1.8 collective-permute-start.10
  185.0 2.6 %collective-permute-start.11 = (f32[64,1024]{1,0:T(8,128)S(1)}, f32[64,1024]{1,0:T(8,128)S(1)}, u32[]{:S(2)}, u32[]{:S(2)}) collective-permute-start(f32[64,1024]{1,0:T(8,128)S(1)} %fusion.201), channel_id=1, source_target_pairs={{0,16},{4,20},{8,24},{12,28},{1,17},{5,21},{9,25},{13,29},{2,18},{... | collective-permute-start | bytes 786440 | tf_op jit(solution)/shard_map/ppermute | solution.py:12
  187.8 7.2 %collective-permute-done.11 = f32[64,1024]{1,0:T(8,128)S(1)} collective-permute-done((f32[64,1024]{1,0:T(8,128)S(1)}, f32[64,1024]{1,0:T(8,128)S(1)}, u32[]{:S(2)}, u32[]{:S(2)}) %collective-permute-start.11) | collective-permute-done | bytes 262176 | tf_op jit(solution)/shard_map/ppermute | solution.py:12
  195.1 5.1 %fusion.68 = f32[128,1024]{1,0:T(8,128)S(1)} fusion(bf16[4,2048,1024]{2,1,0:T(8,128)(2,1)} %param.7, bf16[4,1024,2048]{2,1,0:T(8,128)(2,1)} %param.6, f32[128,1024]{1,0:T(8,128)S(1)} %constant_dynamic-update-slice_fusion, f32[1024]{0:T(1024)S(1)} %bitcast.354, f32[128]{0:T(128)S(1)} %add_rsqrt_fusion.4), kind=kOutput, calls=%fused_computation.68 | convolution fusion | flops 1076494336 | bytes 9441792 | tf_op jit(solution)/shard_map/dot_general | solution.py:21
  200.3 5.2 %fusion.210 = f32[64,1024]{1,0:T(8,128)S(1)} fusion(f32[64,1024]{1,0:T(8,128)S(1)} %fusion.201, bf16[4,2048,1024]{2,1,0:T(8,128)(2,1)} %param.7, bf16[4,1024,2048]{2,1,0:T(8,128)(2,1)} %param.6, f32[64]{0:T(128)S(1)} %add_rsqrt_fusion.6, f32[1024]{0:T(1024)S(1)} %bitcast.340), kind=kOutput, calls=%fused_computation.151 | convolution fusion | flops 538312704 | bytes 9179648 | tf_op jit(solution)/shard_map/dot_general | solution.py:21
  205.6 1.9 collective-permute-start.12
  207.5 4.6 %collective-permute-start.13 = (f32[64,1024]{1,0:T(8,128)S(1)}, f32[64,1024]{1,0:T(8,128)S(1)}, u32[]{:S(2)}, u32[]{:S(2)}) collective-permute-start(f32[64,1024]{1,0:T(8,128)S(1)} %fusion.210), channel_id=1, source_target_pairs={{0,16},{4,20},{8,24},{12,28},{1,17},{5,21},{9,25},{13,29},{2,18},{... | collective-permute-start | bytes 786440 | tf_op jit(solution)/shard_map/ppermute | solution.py:12
  212.2 5.8 %fusion = f32[128,1024]{1,0:T(8,128)} fusion(f32[64,1024]{1,0:T(8,128)S(1)} %get-tuple-element.28, f32[64,1024]{1,0:T(8,128)S(1)} %get-tuple-element.11, f32[1024]{0:T(1024)S(1)} %bitcast.350, f32[128]{0:T(128)S(1)} %add_rsqrt_fusion.1, bf16[4,2048,1024]{2,1,0:T(8,128)(2,1)} %param.7, bf16[4,1024,2048]{2,1,0:T(8,128)(2,1)} %param.6), kind=kOutput, calls=%fused_computation | convolution fusion | flops 1076625408 | bytes 9441792 | tf_op jit(solution)/shard_map/dot_general | solution.py:21
  218.0 1.7 collective-permute-done.13
  219.9 5.0 %fusion.52 = f32[128,1024]{1,0:T(8,128)S(1)} fusion(bf16[4,2048,1024]{2,1,0:T(8,128)(2,1)} %param.7, bf16[4,1024,2048]{2,1,0:T(8,128)(2,1)} %param.6, f32[128,1024]{1,0:T(8,128)S(1)} %constant_dynamic-update-slice_fusion.2, f32[1024]{0:T(1024)S(1)} %bitcast.341, f32[128]{0:T(128)S(1)} %add_rsqrt_fusion.3), kind=kOutput, calls=%fused_computation.52 | convolution fusion | flops 1076494336 | bytes 9441792 | tf_op jit(solution)/shard_map/dot_general | solution.py:21
  225.2 5.2 %fusion.219 = f32[64,1024]{1,0:T(8,128)S(1)} fusion(f32[64,1024]{1,0:T(8,128)S(1)} %fusion.210, bf16[4,2048,1024]{2,1,0:T(8,128)(2,1)} %param.7, bf16[4,1024,2048]{2,1,0:T(8,128)(2,1)} %param.6, f32[64]{0:T(128)S(1)} %add_rsqrt_fusion.5, f32[1024]{0:T(1024)S(1)} %bitcast.336), kind=kOutput, calls=%fused_computation.154 | convolution fusion | flops 538312704 | bytes 9179648 | tf_op jit(solution)/shard_map/dot_general | solution.py:21
  230.4 4.4 %collective-permute-start.15 = (f32[64,1024]{1,0:T(8,128)S(1)}, f32[64,1024]{1,0:T(8,128)S(1)}, u32[]{:S(2)}, u32[]{:S(2)}) collective-permute-start(f32[64,1024]{1,0:T(8,128)S(1)} %fusion.219), channel_id=1, source_target_pairs={{0,16},{4,20},{8,24},{12,28},{1,17},{5,21},{9,25},{13,29},{2,18},{... | collective-permute-start | bytes 786440 | tf_op jit(solution)/shard_map/ppermute | solution.py:12
  234.8 1.7 collective-permute-start.14
  237.6 2.0 pad_maximum_fusion
  239.6 3.7 %collective-permute-done.15 = f32[64,1024]{1,0:T(8,128)S(1)} collective-permute-done((f32[64,1024]{1,0:T(8,128)S(1)}, f32[64,1024]{1,0:T(8,128)S(1)}, u32[]{:S(2)}, u32[]{:S(2)}) %collective-permute-start.15) | collective-permute-done | bytes 262176 | tf_op jit(solution)/shard_map/ppermute | solution.py:12
  243.5 5.9 %fusion.36 = f32[128,1024]{1,0:T(8,128)} fusion(bf16[4,2048,1024]{2,1,0:T(8,128)(2,1)} %param.7, bf16[4,1024,2048]{2,1,0:T(8,128)(2,1)} %param.6, f32[128,1024]{1,0:T(8,128)S(1)} %constant_dynamic-update-slice_fusion.4, f32[1024]{0:T(1024)S(1)} %bitcast.337, f32[128]{0:T(128)S(1)} %add_rsqrt_fusion.2), kind=kOutput, calls=%fused_computation.36 | convolution fusion | flops 1076494336 | bytes 9441792 | tf_op jit(solution)/shard_map/dot_general | solution.py:21
  250.4 1.6 maximum_select_fusion
  (66 shorter events, 13.3 us)
Async XLA Ops:
  8.0 29.2 %copy-start = (f32[64,1024]{1,0:T(8,128)S(1)}, f32[64,1024]{1,0:T(8,128)}, u32[]{:S(2)}) copy-start(f32[64,1024]{1,0:T(8,128)} %param.4) | copy-start | bytes 786436
  24.0 13.3 %collective-permute-start.1 = (f32[64,1024]{1,0:T(8,128)S(1)}, f32[64,1024]{1,0:T(8,128)S(1)}, u32[]{:S(2)}, u32[]{:S(2)}) collective-permute-start(f32[64,1024]{1,0:T(8,128)S(1)} %fusion.120), channel_id=1, source_target_pairs={{0,16},{4,20},{8,24},{12,28},{1,17},{5,21},{9,25},{13,29},{2,18},{... | collective-permute-start | bytes 786440 | tf_op jit(solution)/shard_map/ppermute | solution.py:12
  28.9 8.3 %collective-permute-start = (f32[64,1024]{1,0:T(8,128)S(1)}, f32[64,1024]{1,0:T(8,128)S(1)}, u32[]{:S(2)}, u32[]{:S(2)}) collective-permute-start(f32[64,1024]{1,0:T(8,128)S(1)} %fusion.120), channel_id=1, source_target_pairs={{0,4},{4,8},{8,12},{12,16},{16,20},{20,24},{24,28},{1,5},{5,9},{9,... | collective-permute-start | bytes 786440 | tf_op jit(solution)/shard_map/ppermute | solution.py:12
  59.9 2.4 collective-permute-start.2
  67.7 6.8 %collective-permute-start.3 = (f32[64,1024]{1,0:T(8,128)S(1)}, f32[64,1024]{1,0:T(8,128)S(1)}, u32[]{:S(2)}, u32[]{:S(2)}) collective-permute-start(f32[64,1024]{1,0:T(8,128)S(1)} %fusion.192), channel_id=1, source_target_pairs={{0,4},{4,8},{8,12},{12,16},{16,20},{20,24},{24,28},{1,5},{5,9},{9,... | collective-permute-start | bytes 786440 | tf_op jit(solution)/shard_map/ppermute | solution.py:12
  79.8 7.7 %collective-permute-start.4 = (f32[64,1024]{1,0:T(8,128)S(1)}, f32[64,1024]{1,0:T(8,128)S(1)}, u32[]{:S(2)}, u32[]{:S(2)}) collective-permute-start(f32[64,1024]{1,0:T(8,128)S(1)} %fusion.189), channel_id=1, source_target_pairs={{0,4},{4,8},{8,12},{12,16},{16,20},{20,24},{24,28},{1,5},{5,9},{9,... | collective-permute-start | bytes 786440 | tf_op jit(solution)/shard_map/ppermute | solution.py:12
  92.9 15.4 %collective-permute-start.6 = (f32[64,1024]{1,0:T(8,128)S(1)}, f32[64,1024]{1,0:T(8,128)S(1)}, u32[]{:S(2)}, u32[]{:S(2)}) collective-permute-start(f32[64,1024]{1,0:T(8,128)S(1)} %fusion.186), channel_id=1, source_target_pairs={{0,4},{4,8},{8,12},{12,16},{16,20},{20,24},{24,28},{1,5},{5,9},{9,... | collective-permute-start | bytes 786440 | tf_op jit(solution)/shard_map/ppermute | solution.py:12
  99.4 13.7 %collective-permute-start.5 = (f32[64,1024]{1,0:T(8,128)S(1)}, f32[64,1024]{1,0:T(8,128)S(1)}, u32[]{:S(2)}, u32[]{:S(2)}) collective-permute-start(f32[64,1024]{1,0:T(8,128)S(1)} %fusion.186), channel_id=1, source_target_pairs={{0,16},{4,20},{8,24},{12,28},{1,17},{5,21},{9,25},{13,29},{2,18},{... | collective-permute-start | bytes 786440 | tf_op jit(solution)/shard_map/ppermute | solution.py:12
  118.5 2.4 collective-permute-start.7
  126.3 3.4 %collective-permute-start.8 = (f32[64,1024]{1,0:T(8,128)S(1)}, f32[64,1024]{1,0:T(8,128)S(1)}, u32[]{:S(2)}, u32[]{:S(2)}) collective-permute-start(f32[64,1024]{1,0:T(8,128)S(1)} %fusion.180), channel_id=1, source_target_pairs={{0,4},{4,8},{8,12},{12,16},{16,20},{20,24},{24,28},{1,5},{5,9},{9,... | collective-permute-start | bytes 786440 | tf_op jit(solution)/shard_map/ppermute | solution.py:12
  135.1 42.1 %collective-permute-start.16 = (f32[64,1024]{1,0:T(8,128)S(1)}, f32[64,1024]{1,0:T(8,128)S(1)}, u32[]{:S(2)}, u32[]{:S(2)}) collective-permute-start(f32[64,1024]{1,0:T(8,128)S(1)} %fusion.177), channel_id=1, source_target_pairs={{0,16},{4,20},{8,24},{12,28},{1,17},{5,21},{9,25},{13,29},{2,18},{... | collective-permute-start | bytes 786440 | tf_op jit(solution)/shard_map/ppermute | solution.py:12
  150.9 26.4 %collective-permute-start.9 = (f32[64,1024]{1,0:T(8,128)S(1)}, f32[64,1024]{1,0:T(8,128)S(1)}, u32[]{:S(2)}, u32[]{:S(2)}) collective-permute-start(f32[64,1024]{1,0:T(8,128)S(1)} %fusion.177), channel_id=1, source_target_pairs={{0,4},{4,8},{8,12},{12,16},{16,20},{20,24},{24,28},{1,5},{5,9},{9,... | collective-permute-start | bytes 786440 | tf_op jit(solution)/shard_map/ppermute | solution.py:12
  182.6 5.1 %collective-permute-start.10 = (f32[64,1024]{1,0:T(8,128)S(1)}, f32[64,1024]{1,0:T(8,128)S(1)}, u32[]{:S(2)}, u32[]{:S(2)}) collective-permute-start(f32[64,1024]{1,0:T(8,128)S(1)} %fusion.201), channel_id=1, source_target_pairs={{0,4},{4,8},{8,12},{12,16},{16,20},{20,24},{24,28},{1,5},{5,9},{9,... | collective-permute-start | bytes 786440 | tf_op jit(solution)/shard_map/ppermute | solution.py:12
  185.0 10.0 %collective-permute-start.11 = (f32[64,1024]{1,0:T(8,128)S(1)}, f32[64,1024]{1,0:T(8,128)S(1)}, u32[]{:S(2)}, u32[]{:S(2)}) collective-permute-start(f32[64,1024]{1,0:T(8,128)S(1)} %fusion.201), channel_id=1, source_target_pairs={{0,16},{4,20},{8,24},{12,28},{1,17},{5,21},{9,25},{13,29},{2,18},{... | collective-permute-start | bytes 786440 | tf_op jit(solution)/shard_map/ppermute | solution.py:12
  205.6 19.6 %copy-start.1 = (f32[64,1024]{1,0:T(8,128)}, f32[64,1024]{1,0:T(8,128)S(1)}, u32[]{:S(2)}) copy-start(f32[64,1024]{1,0:T(8,128)S(1)} %fusion.210) | copy-start | bytes 786436
  205.6 12.5 %collective-permute-start.12 = (f32[64,1024]{1,0:T(8,128)S(1)}, f32[64,1024]{1,0:T(8,128)S(1)}, u32[]{:S(2)}, u32[]{:S(2)}) collective-permute-start(f32[64,1024]{1,0:T(8,128)S(1)} %fusion.210), channel_id=1, source_target_pairs={{0,4},{4,8},{8,12},{12,16},{16,20},{20,24},{24,28},{1,5},{5,9},{9,... | collective-permute-start | bytes 786440 | tf_op jit(solution)/shard_map/ppermute | solution.py:12
  207.5 12.3 %collective-permute-start.13 = (f32[64,1024]{1,0:T(8,128)S(1)}, f32[64,1024]{1,0:T(8,128)S(1)}, u32[]{:S(2)}, u32[]{:S(2)}) collective-permute-start(f32[64,1024]{1,0:T(8,128)S(1)} %fusion.210), channel_id=1, source_target_pairs={{0,16},{4,20},{8,24},{12,28},{1,17},{5,21},{9,25},{13,29},{2,18},{... | collective-permute-start | bytes 786440 | tf_op jit(solution)/shard_map/ppermute | solution.py:12
  230.4 12.9 %collective-permute-start.15 = (f32[64,1024]{1,0:T(8,128)S(1)}, f32[64,1024]{1,0:T(8,128)S(1)}, u32[]{:S(2)}, u32[]{:S(2)}) collective-permute-start(f32[64,1024]{1,0:T(8,128)S(1)} %fusion.219), channel_id=1, source_target_pairs={{0,16},{4,20},{8,24},{12,28},{1,17},{5,21},{9,25},{13,29},{2,18},{... | collective-permute-start | bytes 786440 | tf_op jit(solution)/shard_map/ppermute | solution.py:12
  234.8 4.8 %collective-permute-start.14 = (f32[64,1024]{1,0:T(8,128)S(1)}, f32[64,1024]{1,0:T(8,128)S(1)}, u32[]{:S(2)}, u32[]{:S(2)}) collective-permute-start(f32[64,1024]{1,0:T(8,128)S(1)} %fusion.219), channel_id=1, source_target_pairs={{0,4},{4,8},{8,12},{12,16},{16,20},{20,24},{24,28},{1,5},{5,9},{9,... | collective-permute-start | bytes 786440 | tf_op jit(solution)/shard_map/ppermute | solution.py:12
